TPU v7x, 1024 devices: a whole 4x4x32 slice. The times are simulated.
1024 devices in a mesh: gx: 32 (over x, y, core), gy: 8 (over z_lo), gz: 4 (over z_hi).
Axes of the slice: x: 4, y: 4, z: 32 (z_hi: 4, z_lo: 8; z = z_hi * 8 + z_lo), core: 2. Of those that a mesh axis runs over, the one named last changes fastest.
Arguments:
- gas_pos: float32 [3, 32, 8, 4, 2048], P(None, 'gx', 'gy', 'gz'), may hold values from 0 to 1
- gas_mass: float32 [32, 8, 4, 2048], P('gx', 'gy', 'gz'), may hold values from 0.2 to 5
- source_pos: float32 [3, 32, 8, 4, 2048], P(None, 'gx', 'gy', 'gz'), may hold values from 0 to 1
- source_radius: float32 [32, 8, 4, 2048], P('gx', 'gy', 'gz'), may hold values from 0.25 to 1
- source_yield: float32 [2, 32, 8, 4, 2048], P(None, 'gx', 'gy', 'gz'), may hold values from 1 to 30
- source_momentum: float32 [3, 32, 8, 4, 2048], P(None, 'gx', 'gy', 'gz'), may hold values from -180 to 180
- source_tiles: int32 [32, 8, 4, 16, 8], P('gx', 'gy', 'gz'), may hold values from 0 to 431, as said below
- source_count: int32 [32, 8, 4], P('gx', 'gy', 'gz'), may hold values from 1 to 2048, as said below
Outputs:
- gas_gain: float32 [5, 32, 8, 4, 2048], P(None, 'gx', 'gy', 'gz')
Inputs may be any that keep to these rules, and one draw needn't show every extreme that they name: `source_tiles`: the 8 tiles of one block lie one in each of the 8 domains around one corner of the block's domain (that domain among them), in increasing order. Over all blocks of one domain, at most 8 distinct listed tiles lie in any one neighbouring slot. `source_count`: some domain holds 2048 live sources in every draw.
All inputs are finite; a program needn't handle non-finite values.
Results may differ from a plain program's by a relative error of at most 0.0003.
Values sent between devices are 32-bit elements; how exact they have to be, the bound alone decides.
No kernel may reach another device: no remote copies, remote signals or barrier semaphores. Data moves between devices by JAX's collectives and lax.ppermute only.
A program may use at most 32 MiB of HBM per device.

v0:
```python
import math

import jax
import jax.numpy as jnp
from jax import lax
from jax.sharding import PartitionSpec as P


def padded_2(shard, sides, width):
    for axis, dim in sides:
        count, length = (lax.axis_size(axis), shard.shape[dim])
        up = [(i, (i + 1) % count) for i in range(count)]
        down = [(j, i) for i, j in up]
        last = lax.slice_in_dim(shard, length - width, length, axis=dim)
        leading = lax.slice_in_dim(shard, 0, width, axis=dim)
        before = lax.ppermute(last, axis, up)
        after = lax.ppermute(leading, axis, down)
        shard = jnp.concatenate([before, shard, after], axis=dim)
    return shard


def group_deposit(near, tile_ids, source_xyz, inv_square, load, live, tiles_each):
    picked = jnp.take(near, tile_ids, axis=1)
    width = tile_ids.shape[0]
    slot = tile_ids // tiles_each
    shifts = jnp.stack([slot // 9 - 1, slot // 3 % 3 - 1, slot % 3 - 1]).astype(near.dtype)
    gas_xyz = (picked[0:3] + shifts[:, :, :, None]).reshape(3, width, -1)
    masses = picked[3].reshape(width, -1)
    dist_sq = jnp.square(gas_xyz[0][:, None, :] - source_xyz[0][:, :, None])
    dist_sq = dist_sq + jnp.square(gas_xyz[1][:, None, :] - source_xyz[1][:, :, None])
    dist_sq = dist_sq + jnp.square(gas_xyz[2][:, None, :] - source_xyz[2][:, :, None])
    weight = masses[:, None, :] / jnp.square(1.0 + dist_sq * inv_square[:, :, None])
    norm_sum = jnp.sum(weight, axis=2)
    coeffs = load * (live / norm_sum)[None, :, :]
    moved = jnp.einsum("qgs,gsn->qgn", coeffs, weight, precision=lax.Precision.HIGHEST)
    return moved.reshape(load.shape[0], width * tile_ids.shape[1], 128)


def local(
    gas_pos,
    gas_mass,
    source_pos,
    source_radius,
    source_yield,
    source_momentum,
    source_tiles,
    source_count,
):
    gas_size = gas_pos.shape[-1]
    tiles_here = gas_size // 128
    blocks = source_pos.shape[-1] // 128
    listed = source_tiles.shape[-1]
    gas_both = jnp.concatenate([gas_pos, gas_mass[None]], axis=0)
    padded = padded_2(gas_both, (("gx", 1), ("gy", 2), ("gz", 3)), 1)
    near = padded.reshape(4, 27 * tiles_here, 128)
    source_xyz = source_pos.reshape(3, blocks, 128)
    inv_sq = (1.0 / jnp.square(source_radius)).reshape(blocks, 128)
    loads = jnp.concatenate(
        [source_yield[0:1], source_momentum, source_yield[1:2]], axis=0
    ).reshape(5, blocks, 128)
    tile_table = source_tiles.reshape(blocks, listed)
    live_count = source_count.reshape(())
    group = math.gcd(blocks, 4)
    used_blocks = (live_count + 127) // 128
    turns = (used_blocks + group - 1) // group

    def add_group(turn, acc):
        first = turn * group
        live = (
            (first * 128 + lax.iota(jnp.int32, group * 128) < live_count)
            .astype(jnp.float32)
            .reshape(group, 128)
        )
        ids = lax.dynamic_slice_in_dim(tile_table, first, group, 0)
        xyz_rows = lax.dynamic_slice_in_dim(source_xyz, first, group, 1)
        inv_rows = lax.dynamic_slice_in_dim(inv_sq, first, group, 0)
        load_rows = lax.dynamic_slice_in_dim(loads, first, group, 1)
        moved = group_deposit(near, ids, xyz_rows, inv_rows, load_rows, live, tiles_here)
        return acc.at[:, ids.reshape(-1)].add(moved)

    acc_init = jnp.zeros((5, 27 * tiles_here, 128), jnp.float32)
    acc = lax.fori_loop(0, turns, add_group, acc_init)
    spread = acc.reshape(5, 3, 3, 3, gas_size)
    along_z = padded_2(spread, (("gz", 3),), 1)
    partial_z = along_z[:, :, :, 0] + along_z[:, :, :, 2] + along_z[:, :, :, 4]
    along_y = padded_2(partial_z, (("gy", 2),), 1)
    partial_y = along_y[:, :, 0] + along_y[:, :, 2] + along_y[:, :, 4]
    along_x = padded_2(partial_y, (("gx", 1),), 1)
    summed = along_x[:, 0] + along_x[:, 2] + along_x[:, 4]
    gained = summed / gas_mass.reshape(1, gas_size)
    return gained.reshape(5, 1, 1, 1, gas_size)


def solution(mesh):
    in_specs = (
        P(None, "gx", "gy", "gz", None),
        P("gx", "gy", "gz", None),
        P(None, "gx", "gy", "gz", None),
        P("gx", "gy", "gz", None),
        P(None, "gx", "gy", "gz", None),
        P(None, "gx", "gy", "gz", None),
        P("gx", "gy", "gz", None, None),
        P("gx", "gy", "gz"),
    )
    out_specs = P(None, "gx", "gy", "gz", None)
    return jax.shard_map(local, mesh=mesh, in_specs=in_specs, out_specs=out_specs, check_vma=False)
```

profile of v0, /device:TPU:6, one launch (start us, length us, event | category | flops | bytes accessed | tf_op | source)
XLA Modules:
  0.0 214.9 jit_solution(1137863467551757076)
XLA Ops:
  0.0 0.8 pad_maximum_fusion.4
  0.8 4.6 %collective-permute-start.1 = (f32[4,1,1,1,2048]{4,3,2,1,0:T(1,128)S(1)}, f32[4,1,1,1,2048]{4,3,2,1,0:T(1,128)S(1)}, u32[]{:S(2)}, u32[]{:S(2)}) collective-permute-start(f32[4,1,1,1,2048]{4,3,2,1,0:T(1,128)S(1)} %pad_maximum_fusion.4), channel_id=1, source_target_pairs={{32,0},{64,32},{96,64},{128,96},{160,128},{192,160},{224,192},{256... | collective-permute-start | bytes 98312 | tf_op jit(solution)/shard_map/ppermute | solution.py:17
  5.4 1.9 collective-permute-start
  7.4 5.4 %collective-permute-done = f32[4,1,1,1,2048]{4,3,2,1,0:T(1,128)S(1)} collective-permute-done((f32[4,1,1,1,2048]{4,3,2,1,0:T(1,128)S(1)}, f32[4,1,1,1,2048]{4,3,2,1,0:T(1,128)S(1)}, u32[]{:S(2)}, u32[]{:S(2)}) %collective-permute-start) | collective-permute-done | bytes 32800 | tf_op jit(solution)/shard_map/ppermute | solution.py:16
  12.8 0.8 pad_maximum_fusion.2
  13.6 13.2 %collective-permute-start.3 = (f32[4,3,1,1,2048]{4,3,2,1,0:T(1,128)S(1)}, f32[4,3,1,1,2048]{4,3,2,1,0:T(1,128)S(1)}, u32[]{:S(2)}, u32[]{:S(2)}) collective-permute-start(f32[4,3,1,1,2048]{4,3,2,1,0:T(1,128)S(1)} %pad_maximum_fusion.2), channel_id=1, source_target_pairs={{4,0},{8,4},{12,8},{16,12},{20,16},{24,20},{28,24},{0,28},{5,1},{9... | collective-permute-start | bytes 294920 | tf_op jit(solution)/shard_map/ppermute | solution.py:17
  26.8 1.9 collective-permute-start.2
  28.7 0.7 fusion.20
  29.4 19.1 %collective-permute-done.2 = f32[4,3,1,1,2048]{4,3,2,1,0:T(1,128)S(1)} collective-permute-done((f32[4,3,1,1,2048]{4,3,2,1,0:T(1,128)S(1)}, f32[4,3,1,1,2048]{4,3,2,1,0:T(1,128)S(1)}, u32[]{:S(2)}, u32[]{:S(2)}) %collective-permute-start.2) | collective-permute-done | bytes 98336 | tf_op jit(solution)/shard_map/ppermute | solution.py:16
  48.5 1.0 pad_maximum_fusion.1
  49.5 7.4 %collective-permute-start.5 = (f32[4,3,3,1,2048]{4,3,2,1,0:T(1,128)S(1)}, f32[4,3,3,1,2048]{4,3,2,1,0:T(1,128)S(1)}, u32[]{:S(2)}, u32[]{:S(2)}) collective-permute-start(f32[4,3,3,1,2048]{4,3,2,1,0:T(1,128)S(1)} %pad_maximum_fusion.1), channel_id=1, source_target_pairs={{1,0},{2,1},{3,2},{0,3},{5,4},{6,5},{7,6},{4,7},{9,8},{10,9},{11,1... | collective-permute-start | bytes 884744 | tf_op jit(solution)/shard_map/ppermute | solution.py:17
  56.9 8.1 %collective-permute-start.4 = (f32[4,3,3,1,2048]{4,3,2,1,0:T(1,128)S(1)}, f32[4,3,3,1,2048]{4,3,2,1,0:T(1,128)S(1)}, u32[]{:S(2)}, u32[]{:S(2)}) collective-permute-start(f32[4,3,3,1,2048]{4,3,2,1,0:T(1,128)S(1)} %pad_maximum_fusion.1), channel_id=1, source_target_pairs={{0,1},{1,2},{2,3},{3,0},{4,5},{5,6},{6,7},{7,4},{8,9},{9,10},{10,1... | collective-permute-start | bytes 884744 | tf_op jit(solution)/shard_map/ppermute | solution.py:16
  65.0 0.7 multiply_divide_fusion.2
  66.4 0.8 copy.16
  67.2 0.8 pad_maximum_fusion.3
  68.0 20.8 %collective-permute-done.5 = f32[4,3,3,1,2048]{4,3,2,1,0:T(1,128)S(1)} collective-permute-done((f32[4,3,3,1,2048]{4,3,2,1,0:T(1,128)S(1)}, f32[4,3,3,1,2048]{4,3,2,1,0:T(1,128)S(1)}, u32[]{:S(2)}, u32[]{:S(2)}) %collective-permute-start.5) | collective-permute-done | bytes 294944 | tf_op jit(solution)/shard_map/ppermute | solution.py:17
  88.7 11.1 %collective-permute-done.4 = f32[4,3,3,1,2048]{4,3,2,1,0:T(1,128)S(1)} collective-permute-done((f32[4,3,3,1,2048]{4,3,2,1,0:T(1,128)S(1)}, f32[4,3,3,1,2048]{4,3,2,1,0:T(1,128)S(1)}, u32[]{:S(2)}, u32[]{:S(2)}) %collective-permute-start.4) | collective-permute-done | bytes 294944 | tf_op jit(solution)/shard_map/ppermute | solution.py:16
  99.8 1.5 pad_maximum_fusion
  101.3 0.6 reshape.207
  102.0 0.3 copy.17
  102.3 0.1 broadcast_in_dim.34
  102.4 7.9 %while.13 = (s32[]{:T(128)}, f32[5,432,128]{2,0,1:T(8,128)S(1)}, s32[]{:T(128)}, s32[16,8]{1,0:T(8,128)S(1)}, f32[4,432,128]{2,0,1:T(4,128)S(1)}, /*index=5*/f32...) while((s32[]{:T(128)}, f32[5,432,128]{2,0,1:T(8,128)S(1)}, ...), condition=%wide.region_3.4_spmd, body=%wide.region_0.3_spmd.sunk | while | flops 44621864 | bytes 1161807 | solution.py:82
  102.5 0.7 dynamic-slice_bitcast_fusion.4
  103.6 0.6 gather_fusion
  104.4 0.2 slice_reduce_fusion.5
  104.6 1.2 fusion.27
  105.9 0.7 convert_divide_fusion.2
  106.6 2.2 %fusion.28 = f32[4,1024,5]{1,2,0:T(8,128)S(1)} fusion(f32[4,128]{1,0:T(4,128)S(1)} %constant_dynamic-slice_fusion.6, f32[4,128]{1,0:T(4,128)S(1)} %get-tuple-element.301, f32[4,1024]{1,0:T(4,128)S(1)} %bitcast.90, f32[4,128]{1,0:T(4,128)S(1)} %get-tuple-element.307, f32[4,1024]{1,0:T(4,128)S(1)} %bitcast.92, f32[4,128]{1,0:T(4,128)S(1)} %get-tuple-element.309, ...), kind=kOutput, calls=%fused_computation.3.clone.1 | convolution fusion | flops 37751296 | bytes 167936 | tf_op jit(solution)/shard_map/while/body/qgs,gsn->qgn/dot_general | solution.py:35
  108.7 1.6 scatter_fusion
  110.4 0.2 copy.19
  110.6 0.4 reshape.211
  111.0 0.6 fusion.17
  111.6 14.3 %collective-permute-start.6 = (f32[5,3,3,1,2048]{4,3,2,1,0:T(1,128)S(1)}, f32[5,3,3,1,2048]{4,3,2,1,0:T(1,128)S(1)}, u32[]{:S(2)}, u32[]{:S(2)}) collective-permute-start(f32[5,3,3,1,2048]{4,3,2,1,0:T(1,128)S(1)} %get-tuple-element.224), channel_id=1, source_target_pairs={{0,1},{1,2},{2,3},{3,0},{4,5},{5,6},{6,7},{7,4},{8,9},{9,10},{10,1... | collective-permute-start | bytes 1105928 | tf_op jit(solution)/shard_map/ppermute | solution.py:16
  125.9 4.0 %collective-permute-start.7 = (f32[5,3,3,1,2048]{4,3,2,1,0:T(1,128)S(1)}, f32[5,3,3,1,2048]{4,3,2,1,0:T(1,128)S(1)}, u32[]{:S(2)}, u32[]{:S(2)}) collective-permute-start(f32[5,3,3,1,2048]{4,3,2,1,0:T(1,128)S(1)} %get-tuple-element.225), channel_id=1, source_target_pairs={{1,0},{2,1},{3,2},{0,3},{5,4},{6,5},{7,6},{4,7},{9,8},{10,9},{11,1... | collective-permute-start | bytes 1105928 | tf_op jit(solution)/shard_map/ppermute | solution.py:17
  129.9 7.9 %collective-permute-done.6 = f32[5,3,3,1,2048]{4,3,2,1,0:T(1,128)S(1)} collective-permute-done((f32[5,3,3,1,2048]{4,3,2,1,0:T(1,128)S(1)}, f32[5,3,3,1,2048]{4,3,2,1,0:T(1,128)S(1)}, u32[]{:S(2)}, u32[]{:S(2)}) %collective-permute-start.6) | collective-permute-done | bytes 368672 | tf_op jit(solution)/shard_map/ppermute | solution.py:16
  137.8 8.5 %collective-permute-done.7 = f32[5,3,3,1,2048]{4,3,2,1,0:T(1,128)S(1)} collective-permute-done((f32[5,3,3,1,2048]{4,3,2,1,0:T(1,128)S(1)}, f32[5,3,3,1,2048]{4,3,2,1,0:T(1,128)S(1)}, u32[]{:S(2)}, u32[]{:S(2)}) %collective-permute-start.7) | collective-permute-done | bytes 368672 | tf_op jit(solution)/shard_map/ppermute | solution.py:17
  146.3 0.8 fusion.13
  147.2 0.2 copy.40
  147.4 0.2 fusion.18
  147.6 50.1 %collective-permute-start.8 = (f32[5,3,1,2048]{3,2,1,0:T(1,128)S(1)}, f32[5,3,1,2048]{3,2,1,0:T(1,128)S(1)}, u32[]{:S(2)}, u32[]{:S(2)}) collective-permute-start(f32[5,3,1,2048]{3,2,1,0:T(1,128)S(1)} %get-tuple-element.226), channel_id=1, source_target_pairs={{0,4},{4,8},{8,12},{12,16},{16,20},{20,24},{24,28},{28,0},{1,5},{5... | collective-permute-start | bytes 368648 | tf_op jit(solution)/shard_map/ppermute | solution.py:16
  197.7 1.9 collective-permute-start.9
  199.6 0.5 collective-permute-done.8
  200.1 4.4 %collective-permute-done.9 = f32[5,3,1,2048]{3,2,1,0:T(1,128)S(1)} collective-permute-done((f32[5,3,1,2048]{3,2,1,0:T(1,128)S(1)}, f32[5,3,1,2048]{3,2,1,0:T(1,128)S(1)}, u32[]{:S(2)}, u32[]{:S(2)}) %collective-permute-start.9) | collective-permute-done | bytes 122912 | tf_op jit(solution)/shard_map/ppermute | solution.py:17
  204.5 0.3 fusion.14
  204.9 1.9 collective-permute-start.10
  206.8 5.8 %collective-permute-start.11 = (f32[5,1,2048]{2,1,0:T(1,128)S(1)}, f32[5,1,2048]{2,1,0:T(1,128)S(1)}, u32[]{:S(2)}, u32[]{:S(2)}) collective-permute-start(f32[5,1,2048]{2,1,0:T(1,128)S(1)} %get-tuple-element.229), channel_id=1, source_target_pairs={{32,0},{64,32},{96,64},{128,96},{160,128},{192,160},{224,192},{256... | collective-permute-start | bytes 122888 | tf_op jit(solution)/shard_map/ppermute | solution.py:17
  212.6 1.6 collective-permute-done.11
  214.2 0.7 fusion.16
  (25 shorter events, 0.7 us)
Async XLA Ops:
  0.8 6.6 %collective-permute-start.1 = (f32[4,1,1,1,2048]{4,3,2,1,0:T(1,128)S(1)}, f32[4,1,1,1,2048]{4,3,2,1,0:T(1,128)S(1)}, u32[]{:S(2)}, u32[]{:S(2)}) collective-permute-start(f32[4,1,1,1,2048]{4,3,2,1,0:T(1,128)S(1)} %pad_maximum_fusion.4), channel_id=1, source_target_pairs={{32,0},{64,32},{96,64},{128,96},{160,128},{192,160},{224,192},{256... | collective-permute-start | bytes 98312 | tf_op jit(solution)/shard_map/ppermute | solution.py:17
  5.4 7.3 %collective-permute-start = (f32[4,1,1,1,2048]{4,3,2,1,0:T(1,128)S(1)}, f32[4,1,1,1,2048]{4,3,2,1,0:T(1,128)S(1)}, u32[]{:S(2)}, u32[]{:S(2)}) collective-permute-start(f32[4,1,1,1,2048]{4,3,2,1,0:T(1,128)S(1)} %pad_maximum_fusion.4), channel_id=1, source_target_pairs={{0,32},{32,64},{64,96},{96,128},{128,160},{160,192},{192,224},{224... | collective-permute-start | bytes 98312 | tf_op jit(solution)/shard_map/ppermute | solution.py:16
  13.6 15.8 %collective-permute-start.3 = (f32[4,3,1,1,2048]{4,3,2,1,0:T(1,128)S(1)}, f32[4,3,1,1,2048]{4,3,2,1,0:T(1,128)S(1)}, u32[]{:S(2)}, u32[]{:S(2)}) collective-permute-start(f32[4,3,1,1,2048]{4,3,2,1,0:T(1,128)S(1)} %pad_maximum_fusion.2), channel_id=1, source_target_pairs={{4,0},{8,4},{12,8},{16,12},{20,16},{24,20},{28,24},{0,28},{5,1},{9... | collective-permute-start | bytes 294920 | tf_op jit(solution)/shard_map/ppermute | solution.py:17
  26.8 21.7 %collective-permute-start.2 = (f32[4,3,1,1,2048]{4,3,2,1,0:T(1,128)S(1)}, f32[4,3,1,1,2048]{4,3,2,1,0:T(1,128)S(1)}, u32[]{:S(2)}, u32[]{:S(2)}) collective-permute-start(f32[4,3,1,1,2048]{4,3,2,1,0:T(1,128)S(1)} %pad_maximum_fusion.2), channel_id=1, source_target_pairs={{0,4},{4,8},{8,12},{12,16},{16,20},{20,24},{24,28},{28,0},{1,5},{5... | collective-permute-start | bytes 294920 | tf_op jit(solution)/shard_map/ppermute | solution.py:16
  49.5 39.2 %collective-permute-start.5 = (f32[4,3,3,1,2048]{4,3,2,1,0:T(1,128)S(1)}, f32[4,3,3,1,2048]{4,3,2,1,0:T(1,128)S(1)}, u32[]{:S(2)}, u32[]{:S(2)}) collective-permute-start(f32[4,3,3,1,2048]{4,3,2,1,0:T(1,128)S(1)} %pad_maximum_fusion.1), channel_id=1, source_target_pairs={{1,0},{2,1},{3,2},{0,3},{5,4},{6,5},{7,6},{4,7},{9,8},{10,9},{11,1... | collective-permute-start | bytes 884744 | tf_op jit(solution)/shard_map/ppermute | solution.py:17
  56.9 42.9 %collective-permute-start.4 = (f32[4,3,3,1,2048]{4,3,2,1,0:T(1,128)S(1)}, f32[4,3,3,1,2048]{4,3,2,1,0:T(1,128)S(1)}, u32[]{:S(2)}, u32[]{:S(2)}) collective-permute-start(f32[4,3,3,1,2048]{4,3,2,1,0:T(1,128)S(1)} %pad_maximum_fusion.1), channel_id=1, source_target_pairs={{0,1},{1,2},{2,3},{3,0},{4,5},{5,6},{6,7},{7,4},{8,9},{9,10},{10,1... | collective-permute-start | bytes 884744 | tf_op jit(solution)/shard_map/ppermute | solution.py:16
  111.6 26.2 %collective-permute-start.6 = (f32[5,3,3,1,2048]{4,3,2,1,0:T(1,128)S(1)}, f32[5,3,3,1,2048]{4,3,2,1,0:T(1,128)S(1)}, u32[]{:S(2)}, u32[]{:S(2)}) collective-permute-start(f32[5,3,3,1,2048]{4,3,2,1,0:T(1,128)S(1)} %get-tuple-element.224), channel_id=1, source_target_pairs={{0,1},{1,2},{2,3},{3,0},{4,5},{5,6},{6,7},{7,4},{8,9},{9,10},{10,1... | collective-permute-start | bytes 1105928 | tf_op jit(solution)/shard_map/ppermute | solution.py:16
  125.9 88.3 %copy-start = (f32[1,1,1,2048]{3,2,1,0:T(1,128)S(1)}, f32[1,1,1,2048]{3,2,1,0:T(1,128)}, u32[]{:S(2)}) copy-start(f32[1,1,1,2048]{3,2,1,0:T(1,128)} %param.11) | copy-start | bytes 24580
  125.9 20.4 %collective-permute-start.7 = (f32[5,3,3,1,2048]{4,3,2,1,0:T(1,128)S(1)}, f32[5,3,3,1,2048]{4,3,2,1,0:T(1,128)S(1)}, u32[]{:S(2)}, u32[]{:S(2)}) collective-permute-start(f32[5,3,3,1,2048]{4,3,2,1,0:T(1,128)S(1)} %get-tuple-element.225), channel_id=1, source_target_pairs={{1,0},{2,1},{3,2},{0,3},{5,4},{6,5},{7,6},{4,7},{9,8},{10,9},{11,1... | collective-permute-start | bytes 1105928 | tf_op jit(solution)/shard_map/ppermute | solution.py:17
  147.6 52.5 %collective-permute-start.8 = (f32[5,3,1,2048]{3,2,1,0:T(1,128)S(1)}, f32[5,3,1,2048]{3,2,1,0:T(1,128)S(1)}, u32[]{:S(2)}, u32[]{:S(2)}) collective-permute-start(f32[5,3,1,2048]{3,2,1,0:T(1,128)S(1)} %get-tuple-element.226), channel_id=1, source_target_pairs={{0,4},{4,8},{8,12},{12,16},{16,20},{20,24},{24,28},{28,0},{1,5},{5... | collective-permute-start | bytes 368648 | tf_op jit(solution)/shard_map/ppermute | solution.py:16
  197.7 6.8 %collective-permute-start.9 = (f32[5,3,1,2048]{3,2,1,0:T(1,128)S(1)}, f32[5,3,1,2048]{3,2,1,0:T(1,128)S(1)}, u32[]{:S(2)}, u32[]{:S(2)}) collective-permute-start(f32[5,3,1,2048]{3,2,1,0:T(1,128)S(1)} %get-tuple-element.227), channel_id=1, source_target_pairs={{4,0},{8,4},{12,8},{16,12},{20,16},{24,20},{28,24},{0,28},{5,1},{9... | collective-permute-start | bytes 368648 | tf_op jit(solution)/shard_map/ppermute | solution.py:17
  204.9 7.7 %collective-permute-start.10 = (f32[5,1,2048]{2,1,0:T(1,128)S(1)}, f32[5,1,2048]{2,1,0:T(1,128)S(1)}, u32[]{:S(2)}, u32[]{:S(2)}) collective-permute-start(f32[5,1,2048]{2,1,0:T(1,128)S(1)} %get-tuple-element.228), channel_id=1, source_target_pairs={{0,32},{32,64},{64,96},{96,128},{128,160},{160,192},{192,224},{224... | collective-permute-start | bytes 122888 | tf_op jit(solution)/shard_map/ppermute | solution.py:16
  206.8 7.4 %collective-permute-start.11 = (f32[5,1,2048]{2,1,0:T(1,128)S(1)}, f32[5,1,2048]{2,1,0:T(1,128)S(1)}, u32[]{:S(2)}, u32[]{:S(2)}) collective-permute-start(f32[5,1,2048]{2,1,0:T(1,128)S(1)} %get-tuple-element.229), channel_id=1, source_target_pairs={{32,0},{64,32},{96,64},{128,96},{160,128},{192,160},{224,192},{256... | collective-permute-start | bytes 122888 | tf_op jit(solution)/shard_map/ppermute | solution.py:17
where the time goes:
time: 219 us; the launch traced here: 215 us
  starting transfers between devices  115 us (53%)
  waiting for transfers between devices  79.2 us (36%)
  other arithmetic  11.3 us (5%)
  local copies, waits for them, and re-layouts  6.13 us (3%)
    ppermute x6, starting transfers between devices, padded_2(): before = lax.ppermute(last, axis, up)  78.2 us
    ppermute x6, waiting for transfers between devices, padded_2(): before = lax.ppermute(last, axis, up)  43.9 us
    ppermute x6, starting transfers between devices, padded_2(): after = lax.ppermute(leading, axis, down)  36.9 us
    ppermute x6, waiting for transfers between devices, padded_2(): after = lax.ppermute(leading, axis, down)  35.3 us
  transfers between devices with their start and end apart: 12, of which 9 were waited for; matrix products, arithmetic and copies ran while one was open for 1% of the time, Pallas kernels for 0%

commit v1 on v0

--- a/solution.py
+++ b/solution.py
@@ -17,6 +17,15 @@
         after = lax.ppermute(leading, axis, down)
         shard = jnp.concatenate([before, shard, after], axis=dim)
     return shard
+
+
+def folded(slots, axis):
+    count = lax.axis_size(axis)
+    up = [(i, (i + 1) % count) for i in range(count)]
+    down = [(j, i) for i, j in up]
+    before = lax.ppermute(slots[:, 2], axis, up)
+    after = lax.ppermute(slots[:, 0], axis, down)
+    return slots[:, 1] + before + after
 
 
 def group_deposit(near, tile_ids, source_xyz, inv_square, load, live, tiles_each):
@@ -51,7 +60,7 @@
     blocks = source_pos.shape[-1] // 128
     listed = source_tiles.shape[-1]
     gas_both = jnp.concatenate([gas_pos, gas_mass[None]], axis=0)
-    padded = padded_2(gas_both, (("gx", 1), ("gy", 2), ("gz", 3)), 1)
+    padded = padded_2(gas_both, (("gz", 3), ("gy", 2), ("gx", 1)), 1)
     near = padded.reshape(4, 27 * tiles_here, 128)
     source_xyz = source_pos.reshape(3, blocks, 128)
     inv_sq = (1.0 / jnp.square(source_radius)).reshape(blocks, 128)
@@ -81,12 +90,9 @@
     acc_init = jnp.zeros((5, 27 * tiles_here, 128), jnp.float32)
     acc = lax.fori_loop(0, turns, add_group, acc_init)
     spread = acc.reshape(5, 3, 3, 3, gas_size)
-    along_z = padded_2(spread, (("gz", 3),), 1)
-    partial_z = along_z[:, :, :, 0] + along_z[:, :, :, 2] + along_z[:, :, :, 4]
-    along_y = padded_2(partial_z, (("gy", 2),), 1)
-    partial_y = along_y[:, :, 0] + along_y[:, :, 2] + along_y[:, :, 4]
-    along_x = padded_2(partial_y, (("gx", 1),), 1)
-    summed = along_x[:, 0] + along_x[:, 2] + along_x[:, 4]
+    summed = spread
+    for axis in ("gx", "gy", "gz"):
+        summed = folded(summed, axis)
     gained = summed / gas_mass.reshape(1, gas_size)
     return gained.reshape(5, 1, 1, 1, gas_size)
 

time: 219 us -> 162 us (0.74)
  the two profiles are of different devices: /device:TPU:6 before, /device:TPU:31 now
where the time goes in v1:
time: 162 us; the launch traced here: 161 us
  starting transfers between devices  85.5 us (53%)
  waiting for transfers between devices  48.4 us (30%)
  other arithmetic  13.2 us (8%)
  local copies, waits for them, and re-layouts  7.98 us (5%)
  matrix products  4.31 us (3%)
    ppermute x3, starting transfers between devices, padded_2(): after = lax.ppermute(leading, axis, down)  34.5 us
    ppermute x3, starting transfers between devices, folded(): before = lax.ppermute(slots[:, 2], axis, up)  26.6 us
    ppermute x3, waiting for transfers between devices, padded_2(): before = lax.ppermute(last, axis, up)  22.3 us
    ppermute x3, waiting for transfers between devices, folded(): after = lax.ppermute(slots[:, 0], axis, down)  20.9 us
    ppermute x3, starting transfers between devices, folded(): after = lax.ppermute(slots[:, 0], axis, down)  18.1 us
    ppermute x3, starting transfers between devices, padded_2(): before = lax.ppermute(last, axis, up)  6.31 us
    ppermute x3, waiting for transfers between devices, folded(): before = lax.ppermute(slots[:, 2], axis, up)  4.68 us
    dot_general x2, matrix products, group_deposit(): jnp.einsum('qgs,gsn->qgn', coeffs, weight, precision=lax.Precision.HIGHEST)  4.31 us
  transfers between devices with their start and end apart: 12, of which 10 were waited for; matrix products, arithmetic and copies ran while one was open for 2% of the time, Pallas kernels for 0%

profile of v1, /device:TPU:31, one launch (start us, length us, event | category | flops | bytes accessed | tf_op | source)
XLA Modules:
  0.0 160.6 jit_solution(5230193305309577867)
XLA Ops:
  0.0 0.8 pad_maximum_fusion.4
  0.8 22.7 %collective-permute-start.1 = (f32[4,1,1,1,2048]{4,3,2,1,0:T(1,128)S(1)}, f32[4,1,1,1,2048]{4,3,2,1,0:T(1,128)S(1)}, u32[]{:S(2)}, u32[]{:S(2)}) collective-permute-start(f32[4,1,1,1,2048]{4,3,2,1,0:T(1,128)S(1)} %pad_maximum_fusion.4), channel_id=1, source_target_pairs={{1,0},{2,1},{3,2},{0,3},{5,4},{6,5},{7,6},{4,7},{9,8},{10,9},{11,1... | collective-permute-start | bytes 98312 | tf_op jit(solution)/shard_map/ppermute | solution.py:17
  23.5 1.9 %collective-permute-start = (f32[4,1,1,1,2048]{4,3,2,1,0:T(1,128)S(1)}, f32[4,1,1,1,2048]{4,3,2,1,0:T(1,128)S(1)}, u32[]{:S(2)}, u32[]{:S(2)}) collective-permute-start(f32[4,1,1,1,2048]{4,3,2,1,0:T(1,128)S(1)} %pad_maximum_fusion.4), channel_id=1, source_target_pairs={{0,1},{1,2},{2,3},{3,0},{4,5},{5,6},{6,7},{7,4},{8,9},{9,10},{10,1... | collective-permute-start | bytes 98312 | tf_op jit(solution)/shard_map/ppermute | solution.py:16
  25.5 11.5 %collective-permute-done = f32[4,1,1,1,2048]{4,3,2,1,0:T(1,128)S(1)} collective-permute-done((f32[4,1,1,1,2048]{4,3,2,1,0:T(1,128)S(1)}, f32[4,1,1,1,2048]{4,3,2,1,0:T(1,128)S(1)}, u32[]{:S(2)}, u32[]{:S(2)}) %collective-permute-start) | collective-permute-done | bytes 32800 | tf_op jit(solution)/shard_map/ppermute | solution.py:16
  36.9 0.8 pad_maximum_fusion.2
  37.8 5.3 %collective-permute-start.3 = (f32[4,1,1,3,2048]{4,3,2,1,0:T(4,128)S(1)}, f32[4,1,1,3,2048]{4,3,2,1,0:T(4,128)S(1)}, u32[]{:S(2)}, u32[]{:S(2)}) collective-permute-start(f32[4,1,1,3,2048]{4,3,2,1,0:T(4,128)S(1)} %pad_maximum_fusion.2), channel_id=1, source_target_pairs={{4,0},{8,4},{12,8},{16,12},{20,16},{24,20},{28,24},{0,28},{5,1},{9... | collective-permute-start | bytes 294920 | tf_op jit(solution)/shard_map/ppermute | solution.py:17
  43.1 1.9 %collective-permute-start.2 = (f32[4,1,1,3,2048]{4,3,2,1,0:T(4,128)S(1)}, f32[4,1,1,3,2048]{4,3,2,1,0:T(4,128)S(1)}, u32[]{:S(2)}, u32[]{:S(2)}) collective-permute-start(f32[4,1,1,3,2048]{4,3,2,1,0:T(4,128)S(1)} %pad_maximum_fusion.2), channel_id=1, source_target_pairs={{0,4},{4,8},{8,12},{12,16},{16,20},{20,24},{24,28},{28,0},{1,5},{5... | collective-permute-start | bytes 294920 | tf_op jit(solution)/shard_map/ppermute | solution.py:16
  45.0 0.7 fusion.22
  45.8 9.7 %collective-permute-done.2 = f32[4,1,1,3,2048]{4,3,2,1,0:T(4,128)S(1)} collective-permute-done((f32[4,1,1,3,2048]{4,3,2,1,0:T(4,128)S(1)}, f32[4,1,1,3,2048]{4,3,2,1,0:T(4,128)S(1)}, u32[]{:S(2)}, u32[]{:S(2)}) %collective-permute-start.2) | collective-permute-done | bytes 98336 | tf_op jit(solution)/shard_map/ppermute | solution.py:16
  55.4 0.9 pad_maximum_fusion.1
  56.3 6.4 %collective-permute-start.5 = (f32[4,1,3,3,2048]{4,3,2,1,0:T(4,128)S(1)}, f32[4,1,3,3,2048]{4,3,2,1,0:T(4,128)S(1)}, u32[]{:S(2)}, u32[]{:S(2)}) collective-permute-start(f32[4,1,3,3,2048]{4,3,2,1,0:T(4,128)S(1)} %pad_maximum_fusion.1), channel_id=1, source_target_pairs={{32,0},{64,32},{96,64},{128,96},{160,128},{192,160},{224,192},{256... | collective-permute-start | bytes 884744 | tf_op jit(solution)/shard_map/ppermute | solution.py:17
  62.8 2.5 %collective-permute-start.4 = (f32[4,1,3,3,2048]{4,3,2,1,0:T(4,128)S(1)}, f32[4,1,3,3,2048]{4,3,2,1,0:T(4,128)S(1)}, u32[]{:S(2)}, u32[]{:S(2)}) collective-permute-start(f32[4,1,3,3,2048]{4,3,2,1,0:T(4,128)S(1)} %pad_maximum_fusion.1), channel_id=1, source_target_pairs={{0,32},{32,64},{64,96},{96,128},{128,160},{160,192},{192,224},{224... | collective-permute-start | bytes 884744 | tf_op jit(solution)/shard_map/ppermute | solution.py:16
  65.2 0.7 multiply_divide_fusion.2
  66.6 0.8 copy.27
  67.4 0.8 pad_maximum_fusion.3
  68.2 0.6 collective-permute-done.5
  68.8 1.2 collective-permute-done.4
  69.9 1.2 pad_maximum_fusion
  71.2 0.6 reshape.149
  71.8 0.3 copy.28
  72.3 15.9 %while.13 = (s32[]{:T(128)}, f32[5,432,128]{2,0,1:T(8,128)S(1)}, s32[]{:T(128)}, s32[16,8]{1,0:T(8,128)S(1)}, f32[4,432,128]{2,0,1:T(4,128)S(1)}, /*index=5*/f32...) while((s32[]{:T(128)}, f32[5,432,128]{2,0,1:T(8,128)S(1)}, ...), condition=%wide.region_3.4_spmd, body=%wide.region_0.3_spmd.sunk | while | flops 44621864 | bytes 1161807 | solution.py:91
  72.3 0.7 dynamic-slice_bitcast_fusion.4
  73.4 0.6 gather_fusion
  74.5 1.2 fusion.29
  75.7 0.7 convert_divide_fusion.2
  76.4 2.2 %fusion.30 = f32[4,1024,5]{1,2,0:T(8,128)S(1)} fusion(f32[4,128]{1,0:T(4,128)S(1)} %constant_dynamic-slice_fusion.6, f32[4,128]{1,0:T(4,128)S(1)} %get-tuple-element.320, f32[4,1024]{1,0:T(4,128)S(1)} %bitcast.120, f32[4,128]{1,0:T(4,128)S(1)} %get-tuple-element.326, f32[4,1024]{1,0:T(4,128)S(1)} %bitcast.122, f32[4,128]{1,0:T(4,128)S(1)} %get-tuple-element.328, ...), kind=kOutput, calls=%fused_computation.3.clone.1 | convolution fusion | flops 37751296 | bytes 167936 | tf_op jit(solution)/shard_map/while/body/qgs,gsn->qgn/dot_general | solution.py:44
  78.5 1.6 %scatter_fusion = f32[5,432,128]{2,0,1:T(8,128)S(1)} fusion(f32[5,432,128]{2,0,1:T(8,128)S(1)} %get-tuple-element.348, s32[32]{0:T(128)S(1)} %fusion.27, f32[32,5,128]{2,1,0:T(8,128)S(1)} %bitcast.131), kind=kCustom, calls=%fused_computation.1.clone.1 | custom fusion | flops 20480 | bytes 245888 | tf_op jit(solution)/shard_map/while/body/scatter-add | solution.py:88
  80.2 0.7 dynamic-slice_bitcast_fusion.4
  81.3 0.6 gather_fusion
  82.4 1.2 fusion.29
  83.6 0.7 convert_divide_fusion.2
  84.3 2.2 %fusion.30 = f32[4,1024,5]{1,2,0:T(8,128)S(1)} fusion(f32[4,128]{1,0:T(4,128)S(1)} %constant_dynamic-slice_fusion.6, f32[4,128]{1,0:T(4,128)S(1)} %get-tuple-element.320, f32[4,1024]{1,0:T(4,128)S(1)} %bitcast.120, f32[4,128]{1,0:T(4,128)S(1)} %get-tuple-element.326, f32[4,1024]{1,0:T(4,128)S(1)} %bitcast.122, f32[4,128]{1,0:T(4,128)S(1)} %get-tuple-element.328, ...), kind=kOutput, calls=%fused_computation.3.clone.1 | convolution fusion | flops 37751296 | bytes 167936 | tf_op jit(solution)/shard_map/while/body/qgs,gsn->qgn/dot_general | solution.py:44
  86.5 1.6 %scatter_fusion = f32[5,432,128]{2,0,1:T(8,128)S(1)} fusion(f32[5,432,128]{2,0,1:T(8,128)S(1)} %get-tuple-element.348, s32[32]{0:T(128)S(1)} %fusion.27, f32[32,5,128]{2,1,0:T(8,128)S(1)} %bitcast.131), kind=kCustom, calls=%fused_computation.1.clone.1 | custom fusion | flops 20480 | bytes 245888 | tf_op jit(solution)/shard_map/while/body/scatter-add | solution.py:88
  88.1 0.2 copy.30
  88.3 0.4 reshape.153
  88.8 0.3 slice_bitcast_fusion.1
  89.1 15.6 %collective-permute-start.6 = (f32[5,3,3,2048]{3,2,1,0:T(4,128)S(1)}, f32[5,3,3,2048]{3,2,1,0:T(4,128)S(1)}, u32[]{:S(2)}, u32[]{:S(2)}) collective-permute-start(f32[5,3,3,2048]{3,2,1,0:T(4,128)S(1)} %get-tuple-element.242), channel_id=1, source_target_pairs={{0,32},{32,64},{64,96},{96,128},{128,160},{160,192},{192,224},{224... | collective-permute-start | bytes 1105928 | tf_op jit(solution)/shard_map/ppermute | solution.py:26
  104.7 1.9 %collective-permute-start.7 = (f32[5,3,3,2048]{3,2,1,0:T(4,128)S(1)}, f32[5,3,3,2048]{3,2,1,0:T(4,128)S(1)}, u32[]{:S(2)}, u32[]{:S(2)}) collective-permute-start(f32[5,3,3,2048]{3,2,1,0:T(4,128)S(1)} %get-tuple-element.243), channel_id=1, source_target_pairs={{32,0},{64,32},{96,64},{128,96},{160,128},{192,160},{224,192},{256... | collective-permute-start | bytes 1105928 | tf_op jit(solution)/shard_map/ppermute | solution.py:27
  106.7 3.8 %collective-permute-done.6 = f32[5,3,3,2048]{3,2,1,0:T(4,128)S(1)} collective-permute-done((f32[5,3,3,2048]{3,2,1,0:T(4,128)S(1)}, f32[5,3,3,2048]{3,2,1,0:T(4,128)S(1)}, u32[]{:S(2)}, u32[]{:S(2)}) %collective-permute-start.6) | collective-permute-done | bytes 368672 | tf_op jit(solution)/shard_map/ppermute | solution.py:26
  110.5 7.7 %collective-permute-done.7 = f32[5,3,3,2048]{3,2,1,0:T(4,128)S(1)} collective-permute-done((f32[5,3,3,2048]{3,2,1,0:T(4,128)S(1)}, f32[5,3,3,2048]{3,2,1,0:T(4,128)S(1)}, u32[]{:S(2)}, u32[]{:S(2)}) %collective-permute-start.7) | collective-permute-done | bytes 368672 | tf_op jit(solution)/shard_map/ppermute | solution.py:27
  118.5 1.9 %collective-permute-start.8 = (f32[5,3,2048]{2,1,0:T(4,128)S(1)}, f32[5,3,2048]{2,1,0:T(4,128)S(1)}, u32[]{:S(2)}, u32[]{:S(2)}) collective-permute-start(f32[5,3,2048]{2,1,0:T(4,128)S(1)} %get-tuple-element.244), channel_id=1, source_target_pairs={{0,4},{4,8},{8,12},{12,16},{16,20},{20,24},{24,28},{28,0},{1,5},{5... | collective-permute-start | bytes 368648 | tf_op jit(solution)/shard_map/ppermute | solution.py:26
  120.4 10.0 %collective-permute-start.9 = (f32[5,3,2048]{2,1,0:T(4,128)S(1)}, f32[5,3,2048]{2,1,0:T(4,128)S(1)}, u32[]{:S(2)}, u32[]{:S(2)}) collective-permute-start(f32[5,3,2048]{2,1,0:T(4,128)S(1)} %get-tuple-element.245), channel_id=1, source_target_pairs={{4,0},{8,4},{12,8},{16,12},{20,16},{24,20},{28,24},{0,28},{5,1},{9... | collective-permute-start | bytes 368648 | tf_op jit(solution)/shard_map/ppermute | solution.py:27
  130.4 0.8 collective-permute-done.8
  131.1 5.7 %collective-permute-done.9 = f32[5,3,2048]{2,1,0:T(4,128)S(1)} collective-permute-done((f32[5,3,2048]{2,1,0:T(4,128)S(1)}, f32[5,3,2048]{2,1,0:T(4,128)S(1)}, u32[]{:S(2)}, u32[]{:S(2)}) %collective-permute-start.9) | collective-permute-done | bytes 122912 | tf_op jit(solution)/shard_map/ppermute | solution.py:27
  137.1 9.0 %collective-permute-start.10 = (f32[5,2048]{1,0:T(8,128)S(1)}, f32[5,2048]{1,0:T(8,128)S(1)}, u32[]{:S(2)}, u32[]{:S(2)}) collective-permute-start(f32[5,2048]{1,0:T(8,128)S(1)} %bitcast.139), channel_id=1, source_target_pairs={{0,1},{1,2},{2,3},{3,0},{4,5},{5,6},{6,7},{7,4},{8,9},{9,10},{10,1... | collective-permute-start | bytes 122888 | tf_op jit(solution)/shard_map/ppermute | solution.py:26
  146.1 6.2 %collective-permute-start.11 = (f32[5,2048]{1,0:T(8,128)S(1)}, f32[5,2048]{1,0:T(8,128)S(1)}, u32[]{:S(2)}, u32[]{:S(2)}) collective-permute-start(f32[5,2048]{1,0:T(8,128)S(1)} %bitcast.138), channel_id=1, source_target_pairs={{1,0},{2,1},{3,2},{0,3},{5,4},{6,5},{7,6},{4,7},{9,8},{10,9},{11,1... | collective-permute-start | bytes 122888 | tf_op jit(solution)/shard_map/ppermute | solution.py:27
  152.4 7.4 %collective-permute-done.11 = f32[5,2048]{1,0:T(8,128)S(1)} collective-permute-done((f32[5,2048]{1,0:T(8,128)S(1)}, f32[5,2048]{1,0:T(8,128)S(1)}, u32[]{:S(2)}, u32[]{:S(2)}) %collective-permute-start.11) | collective-permute-done | bytes 40992 | tf_op jit(solution)/shard_map/ppermute | solution.py:27
  159.9 0.7 copy.35
  (51 shorter events, 2.2 us)
Async XLA Ops:
  0.8 24.7 %collective-permute-start.1 = (f32[4,1,1,1,2048]{4,3,2,1,0:T(1,128)S(1)}, f32[4,1,1,1,2048]{4,3,2,1,0:T(1,128)S(1)}, u32[]{:S(2)}, u32[]{:S(2)}) collective-permute-start(f32[4,1,1,1,2048]{4,3,2,1,0:T(1,128)S(1)} %pad_maximum_fusion.4), channel_id=1, source_target_pairs={{1,0},{2,1},{3,2},{0,3},{5,4},{6,5},{7,6},{4,7},{9,8},{10,9},{11,1... | collective-permute-start | bytes 98312 | tf_op jit(solution)/shard_map/ppermute | solution.py:17
  23.5 13.4 %collective-permute-start = (f32[4,1,1,1,2048]{4,3,2,1,0:T(1,128)S(1)}, f32[4,1,1,1,2048]{4,3,2,1,0:T(1,128)S(1)}, u32[]{:S(2)}, u32[]{:S(2)}) collective-permute-start(f32[4,1,1,1,2048]{4,3,2,1,0:T(1,128)S(1)} %pad_maximum_fusion.4), channel_id=1, source_target_pairs={{0,1},{1,2},{2,3},{3,0},{4,5},{5,6},{6,7},{7,4},{8,9},{9,10},{10,1... | collective-permute-start | bytes 98312 | tf_op jit(solution)/shard_map/ppermute | solution.py:16
  37.8 8.0 %collective-permute-start.3 = (f32[4,1,1,3,2048]{4,3,2,1,0:T(4,128)S(1)}, f32[4,1,1,3,2048]{4,3,2,1,0:T(4,128)S(1)}, u32[]{:S(2)}, u32[]{:S(2)}) collective-permute-start(f32[4,1,1,3,2048]{4,3,2,1,0:T(4,128)S(1)} %pad_maximum_fusion.2), channel_id=1, source_target_pairs={{4,0},{8,4},{12,8},{16,12},{20,16},{24,20},{28,24},{0,28},{5,1},{9... | collective-permute-start | bytes 294920 | tf_op jit(solution)/shard_map/ppermute | solution.py:17
  43.1 12.3 %collective-permute-start.2 = (f32[4,1,1,3,2048]{4,3,2,1,0:T(4,128)S(1)}, f32[4,1,1,3,2048]{4,3,2,1,0:T(4,128)S(1)}, u32[]{:S(2)}, u32[]{:S(2)}) collective-permute-start(f32[4,1,1,3,2048]{4,3,2,1,0:T(4,128)S(1)} %pad_maximum_fusion.2), channel_id=1, source_target_pairs={{0,4},{4,8},{8,12},{12,16},{16,20},{20,24},{24,28},{28,0},{1,5},{5... | collective-permute-start | bytes 294920 | tf_op jit(solution)/shard_map/ppermute | solution.py:16
  56.3 12.4 %collective-permute-start.5 = (f32[4,1,3,3,2048]{4,3,2,1,0:T(4,128)S(1)}, f32[4,1,3,3,2048]{4,3,2,1,0:T(4,128)S(1)}, u32[]{:S(2)}, u32[]{:S(2)}) collective-permute-start(f32[4,1,3,3,2048]{4,3,2,1,0:T(4,128)S(1)} %pad_maximum_fusion.1), channel_id=1, source_target_pairs={{32,0},{64,32},{96,64},{128,96},{160,128},{192,160},{224,192},{256... | collective-permute-start | bytes 884744 | tf_op jit(solution)/shard_map/ppermute | solution.py:17
  62.8 7.2 %collective-permute-start.4 = (f32[4,1,3,3,2048]{4,3,2,1,0:T(4,128)S(1)}, f32[4,1,3,3,2048]{4,3,2,1,0:T(4,128)S(1)}, u32[]{:S(2)}, u32[]{:S(2)}) collective-permute-start(f32[4,1,3,3,2048]{4,3,2,1,0:T(4,128)S(1)} %pad_maximum_fusion.1), channel_id=1, source_target_pairs={{0,32},{32,64},{64,96},{96,128},{128,160},{160,192},{192,224},{224... | collective-permute-start | bytes 884744 | tf_op jit(solution)/shard_map/ppermute | solution.py:16
  89.1 21.4 %collective-permute-start.6 = (f32[5,3,3,2048]{3,2,1,0:T(4,128)S(1)}, f32[5,3,3,2048]{3,2,1,0:T(4,128)S(1)}, u32[]{:S(2)}, u32[]{:S(2)}) collective-permute-start(f32[5,3,3,2048]{3,2,1,0:T(4,128)S(1)} %get-tuple-element.242), channel_id=1, source_target_pairs={{0,32},{32,64},{64,96},{96,128},{128,160},{160,192},{192,224},{224... | collective-permute-start | bytes 1105928 | tf_op jit(solution)/shard_map/ppermute | solution.py:26
  104.7 55.1 %copy-start = (f32[1,1,1,2048]{3,2,1,0:T(1,128)S(1)}, f32[1,1,1,2048]{3,2,1,0:T(1,128)}, u32[]{:S(2)}) copy-start(f32[1,1,1,2048]{3,2,1,0:T(1,128)} %param.11) | copy-start | bytes 24580
  104.7 13.5 %collective-permute-start.7 = (f32[5,3,3,2048]{3,2,1,0:T(4,128)S(1)}, f32[5,3,3,2048]{3,2,1,0:T(4,128)S(1)}, u32[]{:S(2)}, u32[]{:S(2)}) collective-permute-start(f32[5,3,3,2048]{3,2,1,0:T(4,128)S(1)} %get-tuple-element.243), channel_id=1, source_target_pairs={{32,0},{64,32},{96,64},{128,96},{160,128},{192,160},{224,192},{256... | collective-permute-start | bytes 1105928 | tf_op jit(solution)/shard_map/ppermute | solution.py:27
  118.5 12.7 %collective-permute-start.8 = (f32[5,3,2048]{2,1,0:T(4,128)S(1)}, f32[5,3,2048]{2,1,0:T(4,128)S(1)}, u32[]{:S(2)}, u32[]{:S(2)}) collective-permute-start(f32[5,3,2048]{2,1,0:T(4,128)S(1)} %get-tuple-element.244), channel_id=1, source_target_pairs={{0,4},{4,8},{8,12},{12,16},{16,20},{20,24},{24,28},{28,0},{1,5},{5... | collective-permute-start | bytes 368648 | tf_op jit(solution)/shard_map/ppermute | solution.py:26
  120.4 16.5 %collective-permute-start.9 = (f32[5,3,2048]{2,1,0:T(4,128)S(1)}, f32[5,3,2048]{2,1,0:T(4,128)S(1)}, u32[]{:S(2)}, u32[]{:S(2)}) collective-permute-start(f32[5,3,2048]{2,1,0:T(4,128)S(1)} %get-tuple-element.245), channel_id=1, source_target_pairs={{4,0},{8,4},{12,8},{16,12},{20,16},{24,20},{28,24},{0,28},{5,1},{9... | collective-permute-start | bytes 368648 | tf_op jit(solution)/shard_map/ppermute | solution.py:27
  137.1 15.4 %collective-permute-start.10 = (f32[5,2048]{1,0:T(8,128)S(1)}, f32[5,2048]{1,0:T(8,128)S(1)}, u32[]{:S(2)}, u32[]{:S(2)}) collective-permute-start(f32[5,2048]{1,0:T(8,128)S(1)} %bitcast.139), channel_id=1, source_target_pairs={{0,1},{1,2},{2,3},{3,0},{4,5},{5,6},{6,7},{7,4},{8,9},{9,10},{10,1... | collective-permute-start | bytes 122888 | tf_op jit(solution)/shard_map/ppermute | solution.py:26
  146.1 13.7 %collective-permute-start.11 = (f32[5,2048]{1,0:T(8,128)S(1)}, f32[5,2048]{1,0:T(8,128)S(1)}, u32[]{:S(2)}, u32[]{:S(2)}) collective-permute-start(f32[5,2048]{1,0:T(8,128)S(1)} %bitcast.138), channel_id=1, source_target_pairs={{1,0},{2,1},{3,2},{0,3},{5,4},{6,5},{7,6},{4,7},{9,8},{10,9},{11,1... | collective-permute-start | bytes 122888 | tf_op jit(solution)/shard_map/ppermute | solution.py:27

commit v2 on v0

v2 whole, which is shorter than its diff:
```python
import jax
import jax.numpy as jnp
from jax import lax
from jax.experimental import pallas as pl
from jax.experimental.pallas import tpu as pltpu
from jax.sharding import PartitionSpec as P

TILES = 16
BLOCKS = 16
LISTED = 8
GAS_ROWS = 4 * TILES
TABLE_ROW = GAS_ROWS + 9 * BLOCKS
ROWS = TABLE_ROW + LISTED
DEP_ROWS = 5 * TILES
CAP = 8 * BLOCKS + 2
TOGETHER = 2


def shifted(value, axis, step):
    count = lax.axis_size(axis)
    return lax.ppermute(value, axis, [(i, (i + step) % count) for i in range(count)])


def deposit_kernel(near_ref, far_ref, out_near, out_far, tab_v, tab_s, stage, entries, gas, acc, cols, split, sem):
    packets = [(near_ref if o < 4 else far_ref, (o % 4) * ROWS) for o in range(8)]

    for o, (ref, base) in enumerate(packets):
        ids = ref[pl.ds(base + TABLE_ROW, LISTED), :].astype(jnp.int32)
        word = ids[0:1] & 15
        for j in range(1, LISTED):
            word = word | ((ids[j : j + 1] & 15) << (4 * j))
        lane = lax.broadcasted_iota(jnp.int32, (1, 128), 1)
        tab_v[o : o + 1, :] = word
        tab_v[8 + o : 9 + o, :] = jnp.where(lane < BLOCKS, ids[0:1] >> 4, ids[0:1])
    copy = pltpu.make_async_copy(tab_v, tab_s, sem)
    copy.start()
    acc[...] = jnp.zeros_like(acc)
    for j, (ref, base) in enumerate(packets):
        for axis, bit in enumerate((j // 4, j // 2 % 2, j % 2)):
            rows = ref[pl.ds(base + axis * TILES, TILES), :]
            gas[axis, j * TILES : (j + 1) * TILES, :] = rows + float(bit) if bit else rows
        gas[3, j * TILES : (j + 1) * TILES, :] = ref[pl.ds(base + 3 * TILES, TILES), :]
    copy.wait()

    n = jnp.int32(0)
    for o, (ref, base) in enumerate(packets):
        bits = (o // 4, o // 2 % 2, o % 2)
        wanted = 9 * (1 - bits[0]) + 3 * (1 - bits[1]) + (1 - bits[2])
        count = tab_s[8 + o, BLOCKS]

        def look(b, n, o=o, ref=ref, base=base, bits=bits, wanted=wanted, count=count):
            mine = tab_s[8 + o, b] == wanted

            @pl.when(mine)
            def _():
                first = base + GAS_ROWS + b
                for axis in range(3):
                    row = ref[pl.ds(first + axis * BLOCKS, 1), :]
                    stage[n, axis : axis + 1, :] = row + float(bits[axis]) if bits[axis] else row
                radius = ref[pl.ds(first + 3 * BLOCKS, 1), :]
                stage[n, 3:4, :] = radius * radius
                stage[n, 8:16, :] = jnp.zeros((8, 128), jnp.float32)
                for q in range(5):
                    row = first + (4 + (0, 2, 3, 4, 1)[q]) * BLOCKS
                    stage[n, 8 + q : 9 + q, :] = ref[pl.ds(row, 1), :]
                entries[2 * n] = tab_s[o, b]
                entries[2 * n + 1] = count - 128 * b

            return n + mine.astype(jnp.int32)

        n = lax.fori_loop(0, (count + 127) // 128, look, n)

    @pl.when(n % 2 == 1)
    def _():
        stage[n] = stage[n - 1]
        entries[2 * n] = entries[2 * n - 2]
        entries[2 * n + 1] = 0

    def weights(u, e):
        word = entries[2 * e]
        tiles = [(word >> (4 * j)) & 15 for j in range(LISTED)]
        cols[u] = stage[e].T
        at = [[gas[f, pl.ds(j * TILES + tiles[j], 1), :] for f in range(4)] for j in range(LISTED)]
        norms = []
        for p in range(8):
            x, y, z, r2 = (
                jnp.broadcast_to(cols[u, 16 * p : 16 * p + 16, f : f + 1], (16, 128)) for f in range(4)
            )
            total = None
            for j in range(LISTED):
                dx, dy, dz = at[j][0] - x, at[j][1] - y, at[j][2] - z
                q = dx * dx + dy * dy + (dz * dz + r2)
                k = 1.0 / (q * q)
                mk = at[j][3] * k
                total = mk if total is None else total + mk
                high = k.astype(jnp.bfloat16)
                split[u, 16 * p : 16 * p + 16, 128 * j : 128 * j + 128] = high
                low = (k - high.astype(jnp.float32)).astype(jnp.bfloat16)
                split[u, 128 + 16 * p : 144 + 16 * p, 128 * j : 128 * j + 128] = low
            norms.append(total)
        norm = jnp.sum(jnp.concatenate(norms, axis=0).T, axis=0, keepdims=True)
        return tiles, norm

    def deposits(u, e, norm):
        lane = lax.broadcasted_iota(jnp.int32, (8, 128), 1)
        coeff = jnp.where(lane < entries[2 * e + 1], stage[e, 8:16, :] / norm, 0.0)
        high = coeff.astype(jnp.bfloat16)
        low = (coeff - high.astype(jnp.float32)).astype(jnp.bfloat16)
        left = jnp.concatenate(
            [jnp.concatenate([high, high], axis=1), jnp.concatenate([low, jnp.zeros_like(low)], axis=1)], axis=0
        )
        both = jnp.dot(left, split[u], preferred_element_type=jnp.float32)
        return both[0:8] + both[8:16]

    def turn(i, carry):
        done = [weights(u, TOGETHER * i + u) for u in range(TOGETHER)]
        moved = [deposits(u, TOGETHER * i + u, done[u][1]) for u in range(TOGETHER)]
        for u in range(TOGETHER):
            for j in range(LISTED):
                t = j * TILES + done[u][0][j]
                acc[t] = acc[t] + moved[u][:, 128 * j : 128 * j + 128]
        return carry

    lax.fori_loop(0, (n + TOGETHER - 1) // TOGETHER, turn, 0)
    for o in range(8):
        out = out_near if o < 4 else out_far
        for q in range(5):
            row = (o % 4) * DEP_ROWS + q * TILES
            out[row : row + TILES, :] = acc[o * TILES : (o + 1) * TILES, q, :]


def deposits_of(near, far):
    vmem = pl.BlockSpec(memory_space=pltpu.VMEM)
    out = jax.ShapeDtypeStruct((4 * DEP_ROWS, 128), jnp.float32)
    return pl.pallas_call(
        deposit_kernel,
        out_shape=(out, out),
        in_specs=[vmem, vmem],
        out_specs=(vmem, vmem),
        scratch_shapes=[
            pltpu.VMEM((16, 128), jnp.int32),
            pltpu.SMEM((16, 128), jnp.int32),
            pltpu.VMEM((CAP, 16, 128), jnp.float32),
            pltpu.SMEM((2 * CAP,), jnp.int32),
            pltpu.VMEM((4, 8 * TILES, 128), jnp.float32),
            pltpu.VMEM((8 * TILES, 8, 128), jnp.float32),
            pltpu.VMEM((TOGETHER, 128, 16), jnp.float32),
            pltpu.VMEM((TOGETHER, 256, 1024), jnp.bfloat16),
            pltpu.SemaphoreType.DMA,
        ],
    )(near, far)


def local(gas_pos, gas_mass, source_pos, source_radius, source_yield, source_momentum, source_tiles, source_count):
    table = source_tiles.reshape(BLOCKS, LISTED).T.astype(jnp.float32)
    counts = jnp.broadcast_to(source_count.astype(jnp.float32).reshape(1, 1), (LISTED, 128 - BLOCKS))
    packet = jnp.concatenate(
        [
            gas_pos.reshape(3 * TILES, 128),
            gas_mass.reshape(TILES, 128),
            source_pos.reshape(3 * BLOCKS, 128),
            source_radius.reshape(BLOCKS, 128),
            source_yield.reshape(2 * BLOCKS, 128),
            source_momentum.reshape(3 * BLOCKS, 128),
            jnp.concatenate([table, counts], axis=1),
        ],
        axis=0,
    )
    packet = jnp.concatenate([packet, shifted(packet, "gz", -1)], axis=0)
    packet = jnp.concatenate([packet, shifted(packet, "gy", -1)], axis=0)
    near, far = deposits_of(packet, shifted(packet, "gx", -1))
    total = near + shifted(far, "gx", 1)
    half = 2 * DEP_ROWS
    total = total[:half] + shifted(total[half:], "gy", 1)
    total = total[:DEP_ROWS] + shifted(total[DEP_ROWS:], "gz", 1)
    return total.reshape(5, 1, 1, 1, TILES * 128)


def solution(mesh):
    in_specs = (
        P(None, "gx", "gy", "gz", None),
        P("gx", "gy", "gz", None),
        P(None, "gx", "gy", "gz", None),
        P("gx", "gy", "gz", None),
        P(None, "gx", "gy", "gz", None),
        P(None, "gx", "gy", "gz", None),
        P("gx", "gy", "gz", None, None),
        P("gx", "gy", "gz"),
    )
    out_specs = P(None, "gx", "gy", "gz", None)
    return jax.shard_map(local, mesh=mesh, in_specs=in_specs, out_specs=out_specs, check_vma=False)
```

time: 219 us -> 117 us (0.53); the launches traced: 215 us -> 116 us
  starting transfers between devices: 115 us -> 43.9 us
  waiting for transfers between devices: 79.2 us -> 55.9 us
  other arithmetic: 11.3 us -> 2.27 us
  Pallas kernels: 0 us -> 8.44 us
    ppermute x12 -> x6, starting transfers between devices: 115 us -> 43.9 us  [shifted(): lax.ppermute(value, axis, [(i, (i + step) % count) for i in range(count)])]
    ppermute x12 -> x6, waiting for transfers between devices: 79.2 us -> 55.9 us  [shifted(): lax.ppermute(value, axis, [(i, (i + step) % count) for i in range(count)])]
    pallas_call x0 -> x1, Pallas kernels: none -> 8.44 us  [deposits_of(): pl.pallas_call(deposit_kernel, out_shape=(out, out), in_specs=[vmem, vmem...]
    concatenate x5 -> x0, other arithmetic: 4.96 us -> none  [the longest x3 3.39 us: padded_2(): shard = jnp.concatenate([before, shard, after], axis=dim)]
    unnamed x4 -> x21, local copies, waits for them, and re-layouts: 0.27 us -> 4.4 us
  transfers between devices with their start and end apart: 12 -> 6, of which waited for: 9 -> 6; matrix products, arithmetic and copies ran while one was open for 1% -> 0% of each run, Pallas kernels for 0% -> 0%
where the time goes in v2:
time: 117 us; the launch traced here: 116 us
  waiting for transfers between devices  55.9 us (48%)
  starting transfers between devices  43.9 us (38%)
  Pallas kernels  8.44 us (7%)
  local copies, waits for them, and re-layouts  4.45 us (4%)
  other arithmetic  2.27 us (2%)
    ppermute x6, waiting for transfers between devices, shifted(): lax.ppermute(value, axis, [(i, (i + step) % count) for i in range(count)])  55.9 us
    ppermute x6, starting transfers between devices, shifted(): lax.ppermute(value, axis, [(i, (i + step) % count) for i in range(count)])  43.9 us
    pallas_call x1, Pallas kernels, deposits_of(): pl.pallas_call(deposit_kernel, out_shape=(out, out), in_specs=[vmem, vmem...  8.44 us
    unnamed x21, local copies, waits for them, and re-layouts  4.4 us
  transfers between devices with their start and end apart: 6, of which 6 were waited for; matrix products, arithmetic and copies ran while one was open for 0% of the time, Pallas kernels for 0%

profile of v2, /device:TPU:6, one launch (start us, length us, event | category | flops | bytes accessed | tf_op | source)
XLA Modules:
  0.0 115.7 jit_solution(12683705109740986383)
XLA Ops:
  0.7 0.7 convert_bitcast_fusion
  1.3 0.0 copy-start.5
  1.3 0.8 constant_dynamic-update-slice_fusion.14
  2.1 0.0 copy-start.2
  2.1 0.0 copy-done.5
  2.1 0.7 copy-done.2
  2.8 0.0 copy-start.6
  2.9 0.7 copy-done.6
  3.5 0.0 copy-start.4
  3.5 0.7 copy-done.4
  4.3 0.0 copy-start.3
  4.3 0.7 copy-done.3
  5.0 23.0 %collective-permute-start = (f32[216,128]{1,0:T(8,128)S(1)}, f32[216,128]{1,0:T(8,128)S(1)}, u32[]{:S(2)}, u32[]{:S(2)}) collective-permute-start(f32[216,128]{1,0:T(8,128)S(1)} %get-tuple-element.31), channel_id=1, source_target_pairs={{0,3},{1,0},{2,1},{3,2},{4,7},{5,4},{6,5},{7,6},{8,11},{9,8},{10,9... | collective-permute-start | bytes 331784 | tf_op jit(solution)/shard_map/ppermute | solution.py:21
  28.0 19.1 %collective-permute-done = f32[216,128]{1,0:T(8,128)S(1)} collective-permute-done((f32[216,128]{1,0:T(8,128)S(1)}, f32[216,128]{1,0:T(8,128)S(1)}, u32[]{:S(2)}, u32[]{:S(2)}) %collective-permute-start) | collective-permute-done | bytes 110624 | tf_op jit(solution)/shard_map/ppermute | solution.py:21
  47.2 1.9 %collective-permute-start.1 = (f32[432,128]{1,0:T(8,128)S(1)}, f32[432,128]{1,0:T(8,128)S(1)}, u32[]{:S(2)}, u32[]{:S(2)}) collective-permute-start(f32[432,128]{1,0:T(8,128)S(1)} %get-tuple-element.9), channel_id=1, source_target_pairs={{0,28},{4,0},{8,4},{12,8},{16,12},{20,16},{24,20},{28,24},{1,29},{... | collective-permute-start | bytes 663560 | tf_op jit(solution)/shard_map/ppermute | solution.py:21
  49.1 6.7 %collective-permute-done.1 = f32[432,128]{1,0:T(8,128)S(1)} collective-permute-done((f32[432,128]{1,0:T(8,128)S(1)}, f32[432,128]{1,0:T(8,128)S(1)}, u32[]{:S(2)}, u32[]{:S(2)}) %collective-permute-start.1) | collective-permute-done | bytes 221216 | tf_op jit(solution)/shard_map/ppermute | solution.py:21
  55.8 0.0 copy-start
  55.8 3.3 %collective-permute-start.2 = (f32[864,128]{1,0:T(8,128)S(1)}, f32[864,128]{1,0:T(8,128)S(1)}, u32[]{:S(2)}, u32[]{:S(2)}) collective-permute-start(f32[864,128]{1,0:T(8,128)S(1)} %constant_dynamic-update-slice_fusion.15.near_ref), channel_id=1, source_target_pairs={{0,992},{32,0},{64,32},{96,64},{128,96},{160,128},{192,160},{224,1... | collective-permute-start | bytes 1327112 | tf_op jit(solution)/shard_map/ppermute | solution.py:21
  59.1 5.8 %collective-permute-done.2.far_ref = f32[864,128]{1,0:T(8,128)S(1)} collective-permute-done((f32[864,128]{1,0:T(8,128)S(1)}, f32[864,128]{1,0:T(8,128)S(1)}, u32[]{:S(2)}, u32[]{:S(2)}) %collective-permute-start.2) | collective-permute-done | bytes 442400 | tf_op jit(solution)/shard_map/ppermute | solution.py:21
  64.9 0.0 copy-done
  64.9 0.0 copy-start.1
  64.9 0.8 copy-done.1
  65.6 8.4 %shard_map.82 = (f32[320,128]{1,0:T(8,128)}, f32[320,128]{1,0:T(8,128)}) custom-call(f32[864,128]{1,0:T(8,128)} %copy-done, f32[864,128]{1,0:T(8,128)} %copy-done.1), custom_call_target="tpu_custom_call" | custom-call | tf_op jit(solution)/shard_map/pallas_call | solution.py:135
  74.1 4.6 %collective-permute-start.3 = (f32[320,128]{1,0:T(8,128)}, f32[320,128]{1,0:T(8,128)S(1)}, u32[]{:S(2)}, u32[]{:S(2)}) collective-permute-start(f32[320,128]{1,0:T(8,128)} %get-tuple-element.8), channel_id=1, source_target_pairs={{0,32},{32,64},{64,96},{96,128},{128,160},{160,192},{192,224},{224... | collective-permute-start | bytes 491528 | tf_op jit(solution)/shard_map/ppermute | solution.py:21
  78.7 4.3 %collective-permute-done.3 = f32[320,128]{1,0:T(8,128)S(1)} collective-permute-done((f32[320,128]{1,0:T(8,128)}, f32[320,128]{1,0:T(8,128)S(1)}, u32[]{:S(2)}, u32[]{:S(2)}) %collective-permute-start.3) | collective-permute-done | bytes 163872 | tf_op jit(solution)/shard_map/ppermute | solution.py:21
  83.1 0.9 add.11
  84.0 1.9 %collective-permute-start.4 = (f32[160,128]{1,0:T(8,128)S(1)}, f32[160,128]{1,0:T(8,128)S(1)}, u32[]{:S(2)}, u32[]{:S(2)}) collective-permute-start(f32[160,128]{1,0:T(8,128)S(1)} %slice.17), channel_id=1, source_target_pairs={{0,4},{4,8},{8,12},{12,16},{16,20},{20,24},{24,28},{28,0},{1,5},{5... | collective-permute-start | bytes 245768 | tf_op jit(solution)/shard_map/ppermute | solution.py:21
  85.9 11.9 %collective-permute-done.4 = f32[160,128]{1,0:T(8,128)S(1)} collective-permute-done((f32[160,128]{1,0:T(8,128)S(1)}, f32[160,128]{1,0:T(8,128)S(1)}, u32[]{:S(2)}, u32[]{:S(2)}) %collective-permute-start.4) | collective-permute-done | bytes 81952 | tf_op jit(solution)/shard_map/ppermute | solution.py:21
  97.9 9.1 %collective-permute-start.5 = (f32[80,128]{1,0:T(8,128)S(1)}, f32[80,128]{1,0:T(8,128)S(1)}, u32[]{:S(2)}, u32[]{:S(2)}) collective-permute-start(f32[80,128]{1,0:T(8,128)S(1)} %slice.19), channel_id=1, source_target_pairs={{0,1},{1,2},{2,3},{3,0},{4,5},{5,6},{6,7},{7,4},{8,9},{9,10},{10,1... | collective-permute-start | bytes 122888 | tf_op jit(solution)/shard_map/ppermute | solution.py:21
  107.0 8.0 %collective-permute-done.5 = f32[80,128]{1,0:T(8,128)S(1)} collective-permute-done((f32[80,128]{1,0:T(8,128)S(1)}, f32[80,128]{1,0:T(8,128)S(1)}, u32[]{:S(2)}, u32[]{:S(2)}) %collective-permute-start.5) | collective-permute-done | bytes 40992 | tf_op jit(solution)/shard_map/ppermute | solution.py:21
  115.1 0.6 slice_add_fusion.1
  (11 shorter events, 0.1 us)
Async XLA Ops:
  1.3 0.8 copy-start.5
  2.1 0.7 copy-start.2
  2.8 0.7 copy-start.6
  3.5 0.7 copy-start.4
  4.3 0.7 copy-start.3
  5.0 42.1 %collective-permute-start = (f32[216,128]{1,0:T(8,128)S(1)}, f32[216,128]{1,0:T(8,128)S(1)}, u32[]{:S(2)}, u32[]{:S(2)}) collective-permute-start(f32[216,128]{1,0:T(8,128)S(1)} %get-tuple-element.31), channel_id=1, source_target_pairs={{0,3},{1,0},{2,1},{3,2},{4,7},{5,4},{6,5},{7,6},{8,11},{9,8},{10,9... | collective-permute-start | bytes 331784 | tf_op jit(solution)/shard_map/ppermute | solution.py:21
  47.2 8.6 %collective-permute-start.1 = (f32[432,128]{1,0:T(8,128)S(1)}, f32[432,128]{1,0:T(8,128)S(1)}, u32[]{:S(2)}, u32[]{:S(2)}) collective-permute-start(f32[432,128]{1,0:T(8,128)S(1)} %get-tuple-element.9), channel_id=1, source_target_pairs={{0,28},{4,0},{8,4},{12,8},{16,12},{20,16},{24,20},{28,24},{1,29},{... | collective-permute-start | bytes 663560 | tf_op jit(solution)/shard_map/ppermute | solution.py:21
  55.8 9.1 %copy-start = (f32[864,128]{1,0:T(8,128)}, f32[864,128]{1,0:T(8,128)S(1)}, u32[]{:S(2)}) copy-start(f32[864,128]{1,0:T(8,128)S(1)} %constant_dynamic-update-slice_fusion.15.near_ref) | copy-start | bytes 1327108
  55.8 9.1 %collective-permute-start.2 = (f32[864,128]{1,0:T(8,128)S(1)}, f32[864,128]{1,0:T(8,128)S(1)}, u32[]{:S(2)}, u32[]{:S(2)}) collective-permute-start(f32[864,128]{1,0:T(8,128)S(1)} %constant_dynamic-update-slice_fusion.15.near_ref), channel_id=1, source_target_pairs={{0,992},{32,0},{64,32},{96,64},{128,96},{160,128},{192,160},{224,1... | collective-permute-start | bytes 1327112 | tf_op jit(solution)/shard_map/ppermute | solution.py:21
  64.9 0.8 copy-start.1
  74.1 9.0 %collective-permute-start.3 = (f32[320,128]{1,0:T(8,128)}, f32[320,128]{1,0:T(8,128)S(1)}, u32[]{:S(2)}, u32[]{:S(2)}) collective-permute-start(f32[320,128]{1,0:T(8,128)} %get-tuple-element.8), channel_id=1, source_target_pairs={{0,32},{32,64},{64,96},{96,128},{128,160},{160,192},{192,224},{224... | collective-permute-start | bytes 491528 | tf_op jit(solution)/shard_map/ppermute | solution.py:21
  84.0 13.8 %collective-permute-start.4 = (f32[160,128]{1,0:T(8,128)S(1)}, f32[160,128]{1,0:T(8,128)S(1)}, u32[]{:S(2)}, u32[]{:S(2)}) collective-permute-start(f32[160,128]{1,0:T(8,128)S(1)} %slice.17), channel_id=1, source_target_pairs={{0,4},{4,8},{8,12},{12,16},{16,20},{20,24},{24,28},{28,0},{1,5},{5... | collective-permute-start | bytes 245768 | tf_op jit(solution)/shard_map/ppermute | solution.py:21
  97.9 17.2 %collective-permute-start.5 = (f32[80,128]{1,0:T(8,128)S(1)}, f32[80,128]{1,0:T(8,128)S(1)}, u32[]{:S(2)}, u32[]{:S(2)}) collective-permute-start(f32[80,128]{1,0:T(8,128)S(1)} %slice.19), channel_id=1, source_target_pairs={{0,1},{1,2},{2,3},{3,0},{4,5},{5,6},{6,7},{7,4},{8,9},{9,10},{10,1... | collective-permute-start | bytes 122888 | tf_op jit(solution)/shard_map/ppermute | solution.py:21
